TPU v7x, 256 devices: a whole 4x4x8 slice. The times are simulated.
256 devices in a mesh: row: 32 (over y, z), col: 8 (over x, core).
Axes of the slice: x: 4, y: 4, z: 8, core: 2. Of those that a mesh axis runs over, the one named last changes fastest.
Arguments:
- weights: bfloat16 [2, 8192, 8192], P(None, 'row', 'col'), may hold values from -0.0625 to 0.0625
- preact: float32 [2, 2, 8192], P(None, None, 'row'), may hold values from -2.5 to 2.5
- panel: bfloat16 [2, 64, 8192], P(None, None, 'col'), may hold values from -6 to 6
Outputs:
- basis_out: float32 [2, 64, 8192], P(None, None, 'col')
All inputs are finite; a program needn't handle non-finite values.
Results may differ from a plain program's by a relative error of at most 0.035.
Values may be sent and summed in bfloat16 or wider, within the bound.
No kernel may reach another device: no remote copies, remote signals or barrier semaphores. Data moves between devices by JAX's collectives and lax.ppermute only.
A program may use at most 64 MiB of HBM per device.

v0:
```python
from functools import partial
import jax
import jax.numpy as jnp
from jax import lax
from jax.sharding import PartitionSpec as P

WIDTH = 8192
ITERS = 2


def in_blocks(x, dim, length):
    lengths = x.shape
    tiles = x.reshape(*lengths[:dim], length, lengths[dim] // length, *lengths[dim + 1 :])
    return jnp.moveaxis(tiles, dim, 0)


def sum_at_owner(x, axis, dim):
    tiles = in_blocks(x, dim, lax.axis_size(axis))
    arrived = lax.all_to_all(tiles, axis, split_axis=0, concat_axis=0, tiled=True)
    return arrived.astype(jnp.float32).sum(axis=0)


def from_everyone(x, axis):
    length = lax.axis_size(axis)
    return lax.all_to_all(jnp.broadcast_to(x[None], (length, *x.shape)), axis, 0, 0, tiled=True)


def in_order(tiles, dim):
    tiles = jnp.moveaxis(tiles, 0, dim)
    lengths = tiles.shape
    return tiles.reshape(*lengths[:dim], lengths[dim] * lengths[dim + 1], *lengths[dim + 2 :])


def gathered_copies(x, axis, dim):
    tiles = from_everyone(x, axis)
    return in_order(tiles, dim)


def picked(x, axis, root):
    return lax.dynamic_index_in_dim(lax.all_gather(x, axis), root, 0, keepdims=False)


def over_copies(x, axis):
    everything = from_everyone(x, axis)
    return jnp.sum(everything.astype(jnp.float32), axis=0)


def on_device(weights, preact, panel):
    slopes = 1.0 - jnp.tanh(preact) ** 2
    layers = weights.shape[0]
    span_ratio = lax.axis_size("row") // lax.axis_size("col")
    row_index = lax.axis_index("row")
    current = panel
    basis_out = panel.astype(jnp.float32)
    for iteration in range(ITERS):
        cotangent = None
        for layer_at in range(layers):
            partial_out = jnp.einsum(
                "bki,oi->bko", current, weights[layer_at], preferred_element_type=jnp.float32
            )
            summed = sum_at_owner(partial_out.astype(jnp.bfloat16), "col", 1)
            scaled = (slopes[:, layer_at, None, :] * summed).astype(jnp.bfloat16)
            if layer_at + 1 < layers:
                spread = gathered_copies(scaled, "row", 2)
                current = lax.all_to_all(spread, "col", split_axis=2, concat_axis=1, tiled=True)
            else:
                cotangent = gathered_copies(scaled, "col", 1)
        image_panel = None
        for layer_at in reversed(range(layers)):
            weighted = (slopes[:, layer_at, None, :] * cotangent).astype(jnp.bfloat16)
            partial_in = jnp.einsum(
                "bko,oi->bki", weighted, weights[layer_at], preferred_element_type=jnp.float32
            )
            if layer_at == 0:
                pieces = sum_at_owner(partial_in.astype(jnp.bfloat16), "row", 2).astype(
                    jnp.bfloat16
                )
                image_panel = gathered_copies(pieces, "row", 2)
            else:
                pieces = sum_at_owner(partial_in.astype(jnp.bfloat16), "row", 2).astype(
                    jnp.bfloat16
                )
                gathered = gathered_copies(pieces, "row", 2)
                chosen = picked(gathered, "col", row_index // span_ratio)
                width_row = cotangent.shape[2]
                cotangent = lax.dynamic_slice_in_dim(
                    chosen, row_index % span_ratio * width_row, width_row, 2
                )
        local_gram = jnp.einsum(
            "bkw,bjw->bkj", image_panel, image_panel, preferred_element_type=jnp.float32
        )
        gram_sum = over_copies(local_gram.astype(jnp.bfloat16), "col").astype(jnp.float32)
        factor = jnp.linalg.cholesky(gram_sum / WIDTH)
        basis_out = jax.vmap(partial(jax.scipy.linalg.solve_triangular, lower=True))(
            factor, image_panel.astype(jnp.float32)
        )
        current = basis_out.astype(jnp.bfloat16)
    return basis_out


def solution(mesh):
    return jax.shard_map(
        on_device,
        mesh=mesh,
        in_specs=(P(None, "row", "col"), P(None, None, "row"), P(None, None, "col")),
        out_specs=P(None, None, "col"),
        check_vma=False,
    )
```

profile of v0, /device:TPU:1, one launch (start us, length us, event | category | flops | bytes accessed | tf_op | source)
XLA Modules:
  0.0 452.3 jit_solution(6569241820050055485)
XLA Ops:
  6.5 0.9 copy-done
  7.5 1.3 fusion
  9.5 6.5 %all-to-all-start = ((bf16[8,2,8,256]{3,2,1,0:T(8,128)(2,1)}), bf16[8,2,8,256]{3,2,1,0:T(8,128)(2,1)S(1)}, u32[]{:S(2)}, u32[]{:S(2)}) async-start(bf16[8,2,8,256]{3,2,1,0:T(8,128)(2,1)} %bitcast.159), calls=%async_computation | async-start | bytes 131072 | tf_op jit(solution)/shard_map/all_to_all | solution.py:19
  15.9 0.7 multiply_subtract_fusion
  16.6 4.2 all-to-all-done
  20.9 20.0 %all_to_all.126 = bf16[32,2,8,256]{3,2,1,0:T(8,128)(2,1)S(1)} all-to-all(bf16[32,2,8,256]{3,2,1,0:T(8,128)(2,1)S(1)} %broadcast_in_dim.24), channel_id=1, replica_groups=mesh['row'=32,'col'=8] {'row'}, dimensions={0} | all-to-all | bytes 524288 | tf_op jit(solution)/shard_map/all_to_all | solution.py:25
  40.8 6.8 %copy.135 = bf16[2,8,32,256]{1,0,3,2:T(2,128)(2,1)} copy(bf16[2,8,32,256]{3,1,0,2:T(8,128)(2,1)S(1)} %bitcast.184) | data formatting | bytes 524288 | tf_op jit(solution)/shard_map/reshape | solution.py:31
  47.7 5.8 %reshape.89 = bf16[8,2,8192]{2,1,0:T(2,128)(2,1)S(1)} reshape(bf16[8192,2,8]{2,1,0:T(2,128)(2,1)} %bitcast.166) | data formatting | bytes 524288
  53.4 12.6 %all_to_all.127 = bf16[8,2,8192]{2,1,0:T(2,128)(2,1)S(1)} all-to-all(bf16[8,2,8192]{2,1,0:T(2,128)(2,1)S(1)} %reshape.89), channel_id=1, replica_groups=mesh['row'=32,'col'=8] {'col'}, dimensions={0} | all-to-all | bytes 524288 | tf_op jit(solution)/shard_map/all_to_all | solution.py:65
  66.1 5.9 %reshape.90 = bf16[8192,2,8]{2,1,0:T(2,128)(2,1)} reshape(bf16[8,2,8192]{2,1,0:T(2,128)(2,1)S(1)} %all_to_all.127) | data formatting | bytes 524288
  72.0 9.0 %copy.94 = bf16[2,8,8,1024]{3,1,2,0:T(8,128)(2,1)S(1)} copy(bf16[2,8,8,1024]{1,0,3,2:T(2,128)(2,1)} %bitcast.167) | data formatting | bytes 524288 | tf_op jit(solution)/shard_map/all_to_all | solution.py:65
  81.9 4.3 all-to-all-start.3
  86.2 4.9 %all-to-all-done.3 = bf16[8,2,8,256]{3,2,1,0:T(8,128)(2,1)S(1)} async-done(((bf16[8,2,8,256]{3,2,1,0:T(8,128)(2,1)}), bf16[8,2,8,256]{3,2,1,0:T(8,128)(2,1)S(1)}, u32[]{:S(2)}, u32[]{:S(2)}) %all-to-all-start.3) | async-done | bytes 65568 | tf_op jit(solution)/shard_map/all_to_all | solution.py:19
  91.1 8.0 %all_to_all.128 = bf16[8,2,8,256]{3,2,1,0:T(8,128)(2,1)S(1)} all-to-all(bf16[8,2,8,256]{3,2,1,0:T(8,128)(2,1)S(1)} %broadcast_in_dim.25), channel_id=1, replica_groups=mesh['row'=32,'col'=8] {'col'}, dimensions={0} | all-to-all | bytes 131072 | tf_op jit(solution)/shard_map/all_to_all | solution.py:25
  100.1 13.6 %all_to_all.129 = bf16[32,2,2048]{2,1,0:T(2,128)(2,1)S(1)} all-to-all(bf16[32,2,2048]{2,1,0:T(2,128)(2,1)S(1)} %reshape.91), channel_id=1, replica_groups=mesh['row'=32,'col'=8] {'row'}, dimensions={0} | all-to-all | bytes 524288 | tf_op jit(solution)/shard_map/all_to_all | solution.py:19
  114.7 15.7 %all_to_all.130 = bf16[32,2,2048]{2,1,0:T(2,128)(2,1)S(1)} all-to-all(bf16[32,2,2048]{2,1,0:T(2,128)(2,1)S(1)} %reshape.93), channel_id=1, replica_groups=mesh['row'=32,'col'=8] {'row'}, dimensions={0} | all-to-all | bytes 524288 | tf_op jit(solution)/shard_map/all_to_all | solution.py:25
  130.8 0.9 copy.100
  131.8 25.4 %all-gather.3.cloned.1.call-done = bf16[8,2,64,1024]{3,2,1,0:T(8,128)(2,1)} async-done(((bf16[1,2,64,1024]{3,2,1,0:T(8,128)(2,1)}), bf16[8,2,64,1024]{3,2,1,0:T(8,128)(2,1)}) %all-gather.3.cloned.1.call-update) | async-done | bytes 2097168 | tf_op jit(solution)/shard_map/all_gather | solution.py:40
  157.2 1.2 convolution_convert_fusion.3
  159.1 19.3 %all_to_all.131 = bf16[32,2,2048]{2,1,0:T(2,128)(2,1)S(1)} all-to-all(bf16[32,2,2048]{2,1,0:T(2,128)(2,1)S(1)} %reshape.95), channel_id=1, replica_groups=mesh['row'=32,'col'=8] {'row'}, dimensions={0} | all-to-all | bytes 524288 | tf_op jit(solution)/shard_map/all_to_all | solution.py:19
  179.5 16.1 %all_to_all.132 = bf16[32,2,2048]{2,1,0:T(2,128)(2,1)S(1)} all-to-all(bf16[32,2,2048]{2,1,0:T(2,128)(2,1)S(1)} %reshape.97), channel_id=1, replica_groups=mesh['row'=32,'col'=8] {'row'}, dimensions={0} | all-to-all | bytes 524288 | tf_op jit(solution)/shard_map/all_to_all | solution.py:25
  196.4 0.9 reshape.99
  197.3 7.1 %all-to-all-start.9 = ((bf16[8,2,4096]{2,1,0:T(2,128)(2,1)}), bf16[8,2,4096]{2,1,0:T(2,128)(2,1)S(1)}, u32[]{:S(2)}, u32[]{:S(2)}) async-start(bf16[8,2,4096]{2,1,0:T(2,128)(2,1)} %reshape.99), calls=%async_computation.9 | async-start | bytes 262144 | tf_op jit(solution)/shard_map/all_to_all | solution.py:25
  204.5 5.0 %all-to-all-done.9 = bf16[8,2,4096]{2,1,0:T(2,128)(2,1)S(1)} async-done(((bf16[8,2,4096]{2,1,0:T(2,128)(2,1)}), bf16[8,2,4096]{2,1,0:T(2,128)(2,1)S(1)}, u32[]{:S(2)}, u32[]{:S(2)}) %all-to-all-start.9) | async-done | bytes 131104 | tf_op jit(solution)/shard_map/all_to_all | solution.py:25
  210.0 11.7 %custom-call.8 = f32[2,64,64]{2,1,0:T(8,128)S(1)} custom-call(f32[2,64,64]{2,1,0:T(8,128)S(1)} %fusion.36), custom_call_target="Cholesky" | custom-call | tf_op jit(solution)/shard_map/jit(cholesky)/cholesky | solution.py:93
  222.0 9.8 %custom-call.9 = f32[2,1,64,64]{2,3,1,0:T(8,128)S(1)} custom-call(f32[2,1,64,64]{3,2,1,0:T(8,128)S(1)} %select_bitcast_fusion.1), custom_call_target="InvertDiagBlocksLowerTriangular" | custom-call | tf_op jit(solution)/shard_map/vmap(jit(_solve_triangular))/triangular_solve | solution.py:94
  232.8 8.1 %all_to_all.133 = bf16[8,2,8,256]{3,2,1,0:T(8,128)(2,1)S(1)} all-to-all(bf16[8,2,8,256]{3,2,1,0:T(8,128)(2,1)S(1)} %bitcast.186), channel_id=1, replica_groups=mesh['row'=32,'col'=8] {'col'}, dimensions={0} | all-to-all | bytes 131072 | tf_op jit(solution)/shard_map/all_to_all | solution.py:19
  241.0 13.7 %all_to_all.134 = bf16[32,2,8,256]{3,2,1,0:T(8,128)(2,1)S(1)} all-to-all(bf16[32,2,8,256]{3,2,1,0:T(8,128)(2,1)S(1)} %broadcast_in_dim.29), channel_id=1, replica_groups=mesh['row'=32,'col'=8] {'row'}, dimensions={0} | all-to-all | bytes 524288 | tf_op jit(solution)/shard_map/all_to_all | solution.py:25
  254.6 6.8 %copy.136 = bf16[2,8,32,256]{1,0,3,2:T(2,128)(2,1)} copy(bf16[2,8,32,256]{3,1,0,2:T(8,128)(2,1)S(1)} %bitcast.185) | data formatting | bytes 524288 | tf_op jit(solution)/shard_map/reshape | solution.py:31
  261.4 5.8 %reshape.101 = bf16[8,2,8192]{2,1,0:T(2,128)(2,1)S(1)} reshape(bf16[8192,2,8]{2,1,0:T(2,128)(2,1)} %bitcast.168) | data formatting | bytes 524288
  267.2 12.6 %all_to_all.135 = bf16[8,2,8192]{2,1,0:T(2,128)(2,1)S(1)} all-to-all(bf16[8,2,8192]{2,1,0:T(2,128)(2,1)S(1)} %reshape.101), channel_id=1, replica_groups=mesh['row'=32,'col'=8] {'col'}, dimensions={0} | all-to-all | bytes 524288 | tf_op jit(solution)/shard_map/all_to_all | solution.py:65
  279.8 5.9 %reshape.102 = bf16[8192,2,8]{2,1,0:T(2,128)(2,1)} reshape(bf16[8,2,8192]{2,1,0:T(2,128)(2,1)S(1)} %all_to_all.135) | data formatting | bytes 524288
  285.8 8.9 %copy.113 = bf16[2,8,8,1024]{3,1,2,0:T(8,128)(2,1)S(1)} copy(bf16[2,8,8,1024]{1,0,3,2:T(2,128)(2,1)} %bitcast.169) | data formatting | bytes 524288 | tf_op jit(solution)/shard_map/all_to_all | solution.py:65
  295.0 8.3 %all_to_all.136 = bf16[8,2,8,256]{3,2,1,0:T(8,128)(2,1)S(1)} all-to-all(bf16[8,2,8,256]{3,2,1,0:T(8,128)(2,1)S(1)} %bitcast.187), channel_id=1, replica_groups=mesh['row'=32,'col'=8] {'col'}, dimensions={0} | all-to-all | bytes 131072 | tf_op jit(solution)/shard_map/all_to_all | solution.py:19
  303.3 8.0 %all_to_all.137 = bf16[8,2,8,256]{3,2,1,0:T(8,128)(2,1)S(1)} all-to-all(bf16[8,2,8,256]{3,2,1,0:T(8,128)(2,1)S(1)} %broadcast_in_dim.30), channel_id=1, replica_groups=mesh['row'=32,'col'=8] {'col'}, dimensions={0} | all-to-all | bytes 131072 | tf_op jit(solution)/shard_map/all_to_all | solution.py:25
  312.3 13.6 %all_to_all.138 = bf16[32,2,2048]{2,1,0:T(2,128)(2,1)S(1)} all-to-all(bf16[32,2,2048]{2,1,0:T(2,128)(2,1)S(1)} %reshape.103), channel_id=1, replica_groups=mesh['row'=32,'col'=8] {'row'}, dimensions={0} | all-to-all | bytes 524288 | tf_op jit(solution)/shard_map/all_to_all | solution.py:19
  326.9 15.7 %all_to_all.139 = bf16[32,2,2048]{2,1,0:T(2,128)(2,1)S(1)} all-to-all(bf16[32,2,2048]{2,1,0:T(2,128)(2,1)S(1)} %reshape.105), channel_id=1, replica_groups=mesh['row'=32,'col'=8] {'row'}, dimensions={0} | all-to-all | bytes 524288 | tf_op jit(solution)/shard_map/all_to_all | solution.py:25
  343.0 0.9 copy.119
  343.9 25.5 %all-gather.5.cloned.1.call-done = bf16[8,2,64,1024]{3,2,1,0:T(8,128)(2,1)} async-done(((bf16[1,2,64,1024]{3,2,1,0:T(8,128)(2,1)}), bf16[8,2,64,1024]{3,2,1,0:T(8,128)(2,1)}) %all-gather.5.cloned.1.call-update) | async-done | bytes 2097168 | tf_op jit(solution)/shard_map/all_gather | solution.py:40
  369.4 1.2 convolution_convert_fusion
  371.3 19.3 %all_to_all.140 = bf16[32,2,2048]{2,1,0:T(2,128)(2,1)S(1)} all-to-all(bf16[32,2,2048]{2,1,0:T(2,128)(2,1)S(1)} %reshape.107), channel_id=1, replica_groups=mesh['row'=32,'col'=8] {'row'}, dimensions={0} | all-to-all | bytes 524288 | tf_op jit(solution)/shard_map/all_to_all | solution.py:19
  391.6 16.1 %all_to_all.141 = bf16[32,2,2048]{2,1,0:T(2,128)(2,1)S(1)} all-to-all(bf16[32,2,2048]{2,1,0:T(2,128)(2,1)S(1)} %reshape.109), channel_id=1, replica_groups=mesh['row'=32,'col'=8] {'row'}, dimensions={0} | all-to-all | bytes 524288 | tf_op jit(solution)/shard_map/all_to_all | solution.py:25
  408.5 0.9 reshape.111
  409.4 7.0 %all-to-all-start.19 = ((bf16[8,2,4096]{2,1,0:T(2,128)(2,1)}), bf16[8,2,4096]{2,1,0:T(2,128)(2,1)S(1)}, u32[]{:S(2)}, u32[]{:S(2)}) async-start(bf16[8,2,4096]{2,1,0:T(2,128)(2,1)} %reshape.111), calls=%async_computation.19 | async-start | bytes 262144 | tf_op jit(solution)/shard_map/all_to_all | solution.py:25
  416.7 5.0 %all-to-all-done.19 = bf16[8,2,4096]{2,1,0:T(2,128)(2,1)S(1)} async-done(((bf16[8,2,4096]{2,1,0:T(2,128)(2,1)}), bf16[8,2,4096]{2,1,0:T(2,128)(2,1)S(1)}, u32[]{:S(2)}, u32[]{:S(2)}) %all-to-all-start.19) | async-done | bytes 131104 | tf_op jit(solution)/shard_map/all_to_all | solution.py:25
  422.2 11.7 %custom-call.10 = f32[2,64,64]{2,1,0:T(8,128)S(1)} custom-call(f32[2,64,64]{2,1,0:T(8,128)S(1)} %fusion.34), custom_call_target="Cholesky" | custom-call | tf_op jit(solution)/shard_map/jit(cholesky)/cholesky | solution.py:93
  434.2 9.8 %custom-call.11 = f32[2,1,64,64]{2,3,1,0:T(8,128)S(1)} custom-call(f32[2,1,64,64]{3,2,1,0:T(8,128)S(1)} %select_bitcast_fusion), custom_call_target="InvertDiagBlocksLowerTriangular" | custom-call | tf_op jit(solution)/shard_map/vmap(jit(_solve_triangular))/triangular_solve | solution.py:94
  444.0 1.4 fusion.12
  (98 shorter events, 14.5 us)
Async XLA Ops:
  6.5 1.0 copy-start
  9.5 11.3 %all-to-all-start = ((bf16[8,2,8,256]{3,2,1,0:T(8,128)(2,1)}), bf16[8,2,8,256]{3,2,1,0:T(8,128)(2,1)S(1)}, u32[]{:S(2)}, u32[]{:S(2)}) async-start(bf16[8,2,8,256]{3,2,1,0:T(8,128)(2,1)} %bitcast.159), calls=%async_computation | async-start | bytes 131072 | tf_op jit(solution)/shard_map/all_to_all | solution.py:19
  72.0 9.0 %copy-start.1 = (bf16[2,256,1024]{2,1,0:T(8,128)(2,1)S(1)}, bf16[2,256,1024]{2,1,0:T(8,128)(2,1)}, u32[]{:S(2)}) copy-start(bf16[2,256,1024]{2,1,0:T(8,128)(2,1)} %param.6) | copy-start | bytes 3145732
  81.9 9.2 %all-to-all-start.3 = ((bf16[8,2,8,256]{3,2,1,0:T(8,128)(2,1)}), bf16[8,2,8,256]{3,2,1,0:T(8,128)(2,1)S(1)}, u32[]{:S(2)}, u32[]{:S(2)}) async-start(bf16[8,2,8,256]{3,2,1,0:T(8,128)(2,1)} %bitcast.158), calls=%async_computation.3 | async-start | bytes 131072 | tf_op jit(solution)/shard_map/all_to_all | solution.py:19
  86.2 71.0 %all-gather.3.cloned.1.call-start = ((), (), s32[]{:S(2)}) async-start(), calls=%async_computation.20 | async-start | bytes 2359296 | tf_op jit(solution)/shard_map/all_gather | solution.py:40
  197.3 12.3 %all-to-all-start.9 = ((bf16[8,2,4096]{2,1,0:T(2,128)(2,1)}), bf16[8,2,4096]{2,1,0:T(2,128)(2,1)S(1)}, u32[]{:S(2)}, u32[]{:S(2)}) async-start(bf16[8,2,4096]{2,1,0:T(2,128)(2,1)} %reshape.99), calls=%async_computation.9 | async-start | bytes 262144 | tf_op jit(solution)/shard_map/all_to_all | solution.py:25
  204.3 165.1 %all-gather.5.cloned.1.call-start = ((), (), s32[]{:S(2)}) async-start(), calls=%async_computation.21 | async-start | bytes 2359296 | tf_op jit(solution)/shard_map/all_gather | solution.py:40
  409.4 12.3 %all-to-all-start.19 = ((bf16[8,2,4096]{2,1,0:T(2,128)(2,1)}), bf16[8,2,4096]{2,1,0:T(2,128)(2,1)S(1)}, u32[]{:S(2)}, u32[]{:S(2)}) async-start(bf16[8,2,4096]{2,1,0:T(2,128)(2,1)} %reshape.111), calls=%async_computation.19 | async-start | bytes 262144 | tf_op jit(solution)/shard_map/all_to_all | solution.py:25
Sparse Core Ops, SparseCore 0:
  131.9 25.3 all-gather.2
  344.0 25.3 all-gather.4
where the time goes:
time: 454 us; the launch traced here: 452 us
  blocking collectives  221 us (49%)
  local copies, waits for them, and re-layouts  70 us (15%)
  waiting for transfers between devices  70 us (15%)
  other arithmetic  45 us (10%)
  starting transfers between devices  24.9 us (5%)
  between operations  14.1 us (3%)
  matrix products  7.79 us (2%)
    all_to_all x8, blocking collectives, from_everyone(): lax.all_to_all(jnp.broadcast_to(x[None], (length, *x.shape)), axis, 0, 0,...  113 us
    all_to_all x6, blocking collectives, sum_at_owner(): lax.all_to_all(tiles, axis, split_axis=0, concat_axis=0, tiled=True)  82.2 us
    all_gather x2, waiting for transfers between devices, picked(): lax.all_gather(x, axis)  50.9 us
    unnamed x34, local copies, waits for them, and re-layouts  32.9 us
    all_to_all x2, blocking collectives, on_device(): lax.all_to_all(spread, 'col', split_axis=2, concat_axis=1, tiled=True)  25.2 us
    another operation x7, other arithmetic, on_device(): factor = jnp.linalg.cholesky(gram_sum / WIDTH)  23.8 us
    another operation x5, other arithmetic, on_device(): jax.vmap(partial(jax.scipy.linalg.solve_triangular, lower=True))  19.8 us
    all_to_all x2, local copies, waits for them, and re-layouts, on_device(): lax.all_to_all(spread, 'col', split_axis=2, concat_axis=1, tiled=True)  17.9 us
  transfers between devices with their start and end apart: 6, of which 6 were waited for; matrix products, arithmetic and copies ran while one was open for 0% of the time, Pallas kernels for 0%

commit v1 on v0

--- a/solution.py
+++ b/solution.py
@@ -62,7 +62,9 @@
             scaled = (slopes[:, layer_at, None, :] * summed).astype(jnp.bfloat16)
             if layer_at + 1 < layers:
                 spread = gathered_copies(scaled, "row", 2)
-                current = lax.all_to_all(spread, "col", split_axis=2, concat_axis=1, tiled=True)
+                shards = jnp.split(spread, lax.axis_size("col"), axis=2)
+                incoming = lax.all_to_all(jnp.stack(shards), "col", 0, 0)
+                current = jnp.concatenate(incoming, axis=1)
             else:
                 cotangent = gathered_copies(scaled, "col", 1)
         image_panel = None

time: 454 us -> 399 us (0.88)
  local copies, waits for them, and re-layouts: 70 us -> 15.3 us
    unnamed x34 -> x44, local copies, waits for them, and re-layouts: 32.9 us -> 9.64 us
    all_to_all x2 -> x0, local copies, waits for them, and re-layouts: 17.9 us -> none  [on_device(): lax.all_to_all(spread, 'col', split_axis=2, concat_axis=1, tiled=True)]
    reshape x4, local copies, waits for them, and re-layouts: 14.1 us -> 0.44 us  [in_order(): tiles.reshape(*lengths[:dim], lengths[dim] * lengths[dim + 1], *lengths[d...]
where the time goes in v1:
time: 399 us; the launch traced here: 398 us
  blocking collectives  221 us (55%)
  waiting for transfers between devices  70 us (18%)
  other arithmetic  45 us (11%)
  starting transfers between devices  24.9 us (6%)
  local copies, waits for them, and re-layouts  15.3 us (4%)
  between operations  14.2 us (4%)
  matrix products  7.77 us (2%)
    all_to_all x8, blocking collectives, from_everyone(): lax.all_to_all(jnp.broadcast_to(x[None], (length, *x.shape)), axis, 0, 0,...  113 us
    all_to_all x6, blocking collectives, sum_at_owner(): lax.all_to_all(tiles, axis, split_axis=0, concat_axis=0, tiled=True)  82.2 us
    all_gather x2, waiting for transfers between devices, picked(): lax.all_gather(x, axis)  50.9 us
    all_to_all x2, blocking collectives, on_device(): incoming = lax.all_to_all(jnp.stack(shards), 'col', 0, 0)  25.2 us
    another operation x7, other arithmetic, on_device(): factor = jnp.linalg.cholesky(gram_sum / WIDTH)  23.8 us
    another operation x5, other arithmetic, on_device(): jax.vmap(partial(jax.scipy.linalg.solve_triangular, lower=True))  19.8 us
    all_to_all x2, starting transfers between devices, from_everyone(): lax.all_to_all(jnp.broadcast_to(x[None], (length, *x.shape)), axis, 0, 0,...  14.1 us
    all_to_all x2, starting transfers between devices, sum_at_owner(): lax.all_to_all(tiles, axis, split_axis=0, concat_axis=0, tiled=True)  10.7 us
  transfers between devices with their start and end apart: 6, of which 6 were waited for; matrix products, arithmetic and copies ran while one was open for 0% of the time, Pallas kernels for 0%

profile of v1, /device:TPU:1, one launch (start us, length us, event | category | flops | bytes accessed | tf_op | source)
XLA Modules:
  0.0 397.8 jit_solution(15190778601595388620)
XLA Ops:
  6.5 0.9 copy-done
  7.5 1.3 fusion
  8.8 0.6 copy.188
  9.5 6.5 %all-to-all-start = ((bf16[8,2,8,256]{3,2,1,0:T(8,128)(2,1)}), bf16[8,2,8,256]{3,2,1,0:T(8,128)(2,1)S(1)}, u32[]{:S(2)}, u32[]{:S(2)}) async-start(bf16[8,2,8,256]{3,2,1,0:T(8,128)(2,1)} %bitcast.223), calls=%async_computation | async-start | bytes 131072 | tf_op jit(solution)/shard_map/all_to_all | solution.py:19
  15.9 0.7 multiply_subtract_fusion
  16.6 4.2 %all-to-all-done = bf16[8,2,8,256]{3,2,1,0:T(8,128)(2,1)S(1)} async-done(((bf16[8,2,8,256]{3,2,1,0:T(8,128)(2,1)}), bf16[8,2,8,256]{3,2,1,0:T(8,128)(2,1)S(1)}, u32[]{:S(2)}, u32[]{:S(2)}) %all-to-all-start) | async-done | bytes 65568 | tf_op jit(solution)/shard_map/all_to_all | solution.py:19
  20.9 20.0 %all_to_all.100 = bf16[32,2,8,256]{3,2,1,0:T(8,128)(2,1)S(1)} all-to-all(bf16[32,2,8,256]{3,2,1,0:T(8,128)(2,1)S(1)} %broadcast_in_dim.24), channel_id=1, replica_groups=mesh['row'=32,'col'=8] {'row'}, dimensions={0} | all-to-all | bytes 524288 | tf_op jit(solution)/shard_map/all_to_all | solution.py:25
  41.0 12.6 %all_to_all.101 = bf16[8,2,8,1024]{3,2,1,0:T(8,128)(2,1)S(1)} all-to-all(bf16[8,2,8,1024]{3,2,1,0:T(8,128)(2,1)S(1)} %constant_dynamic-update-slice_fusion), channel_id=1, replica_groups=mesh['row'=32,'col'=8] {'col'}, dimensions={0} | all-to-all | bytes 524288 | tf_op jit(solution)/shard_map/all_to_all | solution.py:66
  53.9 0.6 copy.187
  54.5 4.3 %all-to-all-start.3 = ((bf16[8,2,8,256]{3,2,1,0:T(8,128)(2,1)}), bf16[8,2,8,256]{3,2,1,0:T(8,128)(2,1)S(1)}, u32[]{:S(2)}, u32[]{:S(2)}) async-start(bf16[8,2,8,256]{3,2,1,0:T(8,128)(2,1)} %bitcast.222), calls=%async_computation.3 | async-start | bytes 131072 | tf_op jit(solution)/shard_map/all_to_all | solution.py:19
  58.8 4.9 %all-to-all-done.3 = bf16[8,2,8,256]{3,2,1,0:T(8,128)(2,1)S(1)} async-done(((bf16[8,2,8,256]{3,2,1,0:T(8,128)(2,1)}), bf16[8,2,8,256]{3,2,1,0:T(8,128)(2,1)S(1)}, u32[]{:S(2)}, u32[]{:S(2)}) %all-to-all-start.3) | async-done | bytes 65568 | tf_op jit(solution)/shard_map/all_to_all | solution.py:19
  63.7 8.0 %all_to_all.102 = bf16[8,2,8,256]{3,2,1,0:T(8,128)(2,1)S(1)} all-to-all(bf16[8,2,8,256]{3,2,1,0:T(8,128)(2,1)S(1)} %broadcast_in_dim.25), channel_id=1, replica_groups=mesh['row'=32,'col'=8] {'col'}, dimensions={0} | all-to-all | bytes 131072 | tf_op jit(solution)/shard_map/all_to_all | solution.py:25
  72.3 0.4 reshape.105
  72.7 13.6 %all_to_all.103 = bf16[32,2,2048]{2,1,0:T(2,128)(2,1)S(1)} all-to-all(bf16[32,2,2048]{2,1,0:T(2,128)(2,1)S(1)} %reshape.105), channel_id=1, replica_groups=mesh['row'=32,'col'=8] {'row'}, dimensions={0} | all-to-all | bytes 524288 | tf_op jit(solution)/shard_map/all_to_all | solution.py:19
  86.9 0.4 reshape.107
  87.3 15.7 %all_to_all.104 = bf16[32,2,2048]{2,1,0:T(2,128)(2,1)S(1)} all-to-all(bf16[32,2,2048]{2,1,0:T(2,128)(2,1)S(1)} %reshape.107), channel_id=1, replica_groups=mesh['row'=32,'col'=8] {'row'}, dimensions={0} | all-to-all | bytes 524288 | tf_op jit(solution)/shard_map/all_to_all | solution.py:25
  103.4 0.9 copy.121
  104.4 25.4 %all-gather.3.cloned.1.call-done = bf16[8,2,64,1024]{3,2,1,0:T(8,128)(2,1)} async-done(((bf16[1,2,64,1024]{3,2,1,0:T(8,128)(2,1)}), bf16[8,2,64,1024]{3,2,1,0:T(8,128)(2,1)}) %all-gather.3.cloned.1.call-update) | async-done | bytes 2097168 | tf_op jit(solution)/shard_map/all_gather | solution.py:40
  129.8 1.2 convolution_convert_fusion.3
  131.4 0.4 reshape.109
  131.8 19.3 %all_to_all.105 = bf16[32,2,2048]{2,1,0:T(2,128)(2,1)S(1)} all-to-all(bf16[32,2,2048]{2,1,0:T(2,128)(2,1)S(1)} %reshape.109), channel_id=1, replica_groups=mesh['row'=32,'col'=8] {'row'}, dimensions={0} | all-to-all | bytes 524288 | tf_op jit(solution)/shard_map/all_to_all | solution.py:19
  152.1 16.1 %all_to_all.106 = bf16[32,2,2048]{2,1,0:T(2,128)(2,1)S(1)} all-to-all(bf16[32,2,2048]{2,1,0:T(2,128)(2,1)S(1)} %reshape.111), channel_id=1, replica_groups=mesh['row'=32,'col'=8] {'row'}, dimensions={0} | all-to-all | bytes 524288 | tf_op jit(solution)/shard_map/all_to_all | solution.py:25
  169.0 0.9 reshape.113
  169.9 7.0 %all-to-all-start.9 = ((bf16[8,2,4096]{2,1,0:T(2,128)(2,1)}), bf16[8,2,4096]{2,1,0:T(2,128)(2,1)S(1)}, u32[]{:S(2)}, u32[]{:S(2)}) async-start(bf16[8,2,4096]{2,1,0:T(2,128)(2,1)} %reshape.113), calls=%async_computation.9 | async-start | bytes 262144 | tf_op jit(solution)/shard_map/all_to_all | solution.py:25
  177.2 5.0 %all-to-all-done.9 = bf16[8,2,4096]{2,1,0:T(2,128)(2,1)S(1)} async-done(((bf16[8,2,4096]{2,1,0:T(2,128)(2,1)}), bf16[8,2,4096]{2,1,0:T(2,128)(2,1)S(1)}, u32[]{:S(2)}, u32[]{:S(2)}) %all-to-all-start.9) | async-done | bytes 131104 | tf_op jit(solution)/shard_map/all_to_all | solution.py:25
  182.7 11.7 %custom-call.8 = f32[2,64,64]{2,1,0:T(8,128)S(1)} custom-call(f32[2,64,64]{2,1,0:T(8,128)S(1)} %fusion.38), custom_call_target="Cholesky" | custom-call | tf_op jit(solution)/shard_map/jit(cholesky)/cholesky | solution.py:95
  194.7 9.8 %custom-call.9 = f32[2,1,64,64]{2,3,1,0:T(8,128)S(1)} custom-call(f32[2,1,64,64]{3,2,1,0:T(8,128)S(1)} %select_bitcast_fusion.1), custom_call_target="InvertDiagBlocksLowerTriangular" | custom-call | tf_op jit(solution)/shard_map/vmap(jit(_solve_triangular))/triangular_solve | solution.py:96
  204.5 0.6 convolution_convert_fusion.2
  205.5 8.1 %all_to_all.107 = bf16[8,2,8,256]{3,2,1,0:T(8,128)(2,1)S(1)} all-to-all(bf16[8,2,8,256]{3,2,1,0:T(8,128)(2,1)S(1)} %bitcast.262), channel_id=1, replica_groups=mesh['row'=32,'col'=8] {'col'}, dimensions={0} | all-to-all | bytes 131072 | tf_op jit(solution)/shard_map/all_to_all | solution.py:19
  213.6 13.8 %all_to_all.108 = bf16[32,2,8,256]{3,2,1,0:T(8,128)(2,1)S(1)} all-to-all(bf16[32,2,8,256]{3,2,1,0:T(8,128)(2,1)S(1)} %broadcast_in_dim.29), channel_id=1, replica_groups=mesh['row'=32,'col'=8] {'row'}, dimensions={0} | all-to-all | bytes 524288 | tf_op jit(solution)/shard_map/all_to_all | solution.py:25
  227.6 12.6 %all_to_all.109 = bf16[8,2,8,1024]{3,2,1,0:T(8,128)(2,1)S(1)} all-to-all(bf16[8,2,8,1024]{3,2,1,0:T(8,128)(2,1)S(1)} %constant_dynamic-update-slice_fusion.8), channel_id=1, replica_groups=mesh['row'=32,'col'=8] {'col'}, dimensions={0} | all-to-all | bytes 524288 | tf_op jit(solution)/shard_map/all_to_all | solution.py:66
  240.5 8.3 %all_to_all.110 = bf16[8,2,8,256]{3,2,1,0:T(8,128)(2,1)S(1)} all-to-all(bf16[8,2,8,256]{3,2,1,0:T(8,128)(2,1)S(1)} %bitcast.263), channel_id=1, replica_groups=mesh['row'=32,'col'=8] {'col'}, dimensions={0} | all-to-all | bytes 131072 | tf_op jit(solution)/shard_map/all_to_all | solution.py:19
  248.8 8.0 %all_to_all.111 = bf16[8,2,8,256]{3,2,1,0:T(8,128)(2,1)S(1)} all-to-all(bf16[8,2,8,256]{3,2,1,0:T(8,128)(2,1)S(1)} %broadcast_in_dim.30), channel_id=1, replica_groups=mesh['row'=32,'col'=8] {'col'}, dimensions={0} | all-to-all | bytes 131072 | tf_op jit(solution)/shard_map/all_to_all | solution.py:25
  257.4 0.4 reshape.115
  257.8 13.6 %all_to_all.112 = bf16[32,2,2048]{2,1,0:T(2,128)(2,1)S(1)} all-to-all(bf16[32,2,2048]{2,1,0:T(2,128)(2,1)S(1)} %reshape.115), channel_id=1, replica_groups=mesh['row'=32,'col'=8] {'row'}, dimensions={0} | all-to-all | bytes 524288 | tf_op jit(solution)/shard_map/all_to_all | solution.py:19
  272.0 0.4 reshape.117
  272.4 15.7 %all_to_all.113 = bf16[32,2,2048]{2,1,0:T(2,128)(2,1)S(1)} all-to-all(bf16[32,2,2048]{2,1,0:T(2,128)(2,1)S(1)} %reshape.117), channel_id=1, replica_groups=mesh['row'=32,'col'=8] {'row'}, dimensions={0} | all-to-all | bytes 524288 | tf_op jit(solution)/shard_map/all_to_all | solution.py:25
  288.5 0.9 copy.139
  289.4 25.5 %all-gather.5.cloned.1.call-done = bf16[8,2,64,1024]{3,2,1,0:T(8,128)(2,1)} async-done(((bf16[1,2,64,1024]{3,2,1,0:T(8,128)(2,1)}), bf16[8,2,64,1024]{3,2,1,0:T(8,128)(2,1)}) %all-gather.5.cloned.1.call-update) | async-done | bytes 2097168 | tf_op jit(solution)/shard_map/all_gather | solution.py:40
  314.9 1.2 convolution_convert_fusion
  316.8 19.3 %all_to_all.114 = bf16[32,2,2048]{2,1,0:T(2,128)(2,1)S(1)} all-to-all(bf16[32,2,2048]{2,1,0:T(2,128)(2,1)S(1)} %reshape.119), channel_id=1, replica_groups=mesh['row'=32,'col'=8] {'row'}, dimensions={0} | all-to-all | bytes 524288 | tf_op jit(solution)/shard_map/all_to_all | solution.py:19
  337.1 16.1 %all_to_all.115 = bf16[32,2,2048]{2,1,0:T(2,128)(2,1)S(1)} all-to-all(bf16[32,2,2048]{2,1,0:T(2,128)(2,1)S(1)} %reshape.121), channel_id=1, replica_groups=mesh['row'=32,'col'=8] {'row'}, dimensions={0} | all-to-all | bytes 524288 | tf_op jit(solution)/shard_map/all_to_all | solution.py:25
  354.1 0.9 reshape.123
  355.0 7.1 %all-to-all-start.19 = ((bf16[8,2,4096]{2,1,0:T(2,128)(2,1)}), bf16[8,2,4096]{2,1,0:T(2,128)(2,1)S(1)}, u32[]{:S(2)}, u32[]{:S(2)}) async-start(bf16[8,2,4096]{2,1,0:T(2,128)(2,1)} %reshape.123), calls=%async_computation.19 | async-start | bytes 262144 | tf_op jit(solution)/shard_map/all_to_all | solution.py:25
  362.2 5.0 %all-to-all-done.19 = bf16[8,2,4096]{2,1,0:T(2,128)(2,1)S(1)} async-done(((bf16[8,2,4096]{2,1,0:T(2,128)(2,1)}), bf16[8,2,4096]{2,1,0:T(2,128)(2,1)S(1)}, u32[]{:S(2)}, u32[]{:S(2)}) %all-to-all-start.19) | async-done | bytes 131104 | tf_op jit(solution)/shard_map/all_to_all | solution.py:25
  367.7 11.7 %custom-call.10 = f32[2,64,64]{2,1,0:T(8,128)S(1)} custom-call(f32[2,64,64]{2,1,0:T(8,128)S(1)} %fusion.36), custom_call_target="Cholesky" | custom-call | tf_op jit(solution)/shard_map/jit(cholesky)/cholesky | solution.py:95
  379.7 9.8 %custom-call.11 = f32[2,1,64,64]{2,3,1,0:T(8,128)S(1)} custom-call(f32[2,1,64,64]{3,2,1,0:T(8,128)S(1)} %select_bitcast_fusion), custom_call_target="InvertDiagBlocksLowerTriangular" | custom-call | tf_op jit(solution)/shard_map/vmap(jit(_solve_triangular))/triangular_solve | solution.py:96
  389.5 1.4 fusion.12
  (108 shorter events, 10.7 us)
Async XLA Ops:
  6.5 1.0 copy-start
  6.5 47.0 %copy-start.1 = (bf16[2,256,1024]{2,1,0:T(8,128)(2,1)S(1)}, bf16[2,256,1024]{2,1,0:T(8,128)(2,1)}, u32[]{:S(2)}) copy-start(bf16[2,256,1024]{2,1,0:T(8,128)(2,1)} %param.6) | copy-start | bytes 3145732
  9.5 11.3 %all-to-all-start = ((bf16[8,2,8,256]{3,2,1,0:T(8,128)(2,1)}), bf16[8,2,8,256]{3,2,1,0:T(8,128)(2,1)S(1)}, u32[]{:S(2)}, u32[]{:S(2)}) async-start(bf16[8,2,8,256]{3,2,1,0:T(8,128)(2,1)} %bitcast.223), calls=%async_computation | async-start | bytes 131072 | tf_op jit(solution)/shard_map/all_to_all | solution.py:19
  54.5 9.2 %all-to-all-start.3 = ((bf16[8,2,8,256]{3,2,1,0:T(8,128)(2,1)}), bf16[8,2,8,256]{3,2,1,0:T(8,128)(2,1)S(1)}, u32[]{:S(2)}, u32[]{:S(2)}) async-start(bf16[8,2,8,256]{3,2,1,0:T(8,128)(2,1)} %bitcast.222), calls=%async_computation.3 | async-start | bytes 131072 | tf_op jit(solution)/shard_map/all_to_all | solution.py:19
  58.8 71.0 %all-gather.3.cloned.1.call-start = ((), (), s32[]{:S(2)}) async-start(), calls=%async_computation.20 | async-start | bytes 2359296 | tf_op jit(solution)/shard_map/all_gather | solution.py:40
  169.9 12.3 %all-to-all-start.9 = ((bf16[8,2,4096]{2,1,0:T(2,128)(2,1)}), bf16[8,2,4096]{2,1,0:T(2,128)(2,1)S(1)}, u32[]{:S(2)}, u32[]{:S(2)}) async-start(bf16[8,2,4096]{2,1,0:T(2,128)(2,1)} %reshape.113), calls=%async_computation.9 | async-start | bytes 262144 | tf_op jit(solution)/shard_map/all_to_all | solution.py:25
  177.0 138.0 %all-gather.5.cloned.1.call-start = ((), (), s32[]{:S(2)}) async-start(), calls=%async_computation.21 | async-start | bytes 2359296 | tf_op jit(solution)/shard_map/all_gather | solution.py:40
  355.0 12.3 %all-to-all-start.19 = ((bf16[8,2,4096]{2,1,0:T(2,128)(2,1)}), bf16[8,2,4096]{2,1,0:T(2,128)(2,1)S(1)}, u32[]{:S(2)}, u32[]{:S(2)}) async-start(bf16[8,2,4096]{2,1,0:T(2,128)(2,1)} %reshape.123), calls=%async_computation.19 | async-start | bytes 262144 | tf_op jit(solution)/shard_map/all_to_all | solution.py:25
Sparse Core Ops, SparseCore 0:
  104.5 25.3 all-gather.2
  289.6 25.3 all-gather.4
